TPU v7x, 256 devices: a whole 4x4x8 slice. The times are simulated.
256 devices in a mesh: blk: 16 (over x, y_hi, core), grp: 16 (over y_lo, z).
Axes of the slice: x: 4, y: 4 (y_hi: 2, y_lo: 2; y = y_hi * 2 + y_lo), z: 8, core: 2. Of those that a mesh axis runs over, the one named last changes fastest.
Arguments:
- amplitudes: bfloat16 [896, 4, 896], P('blk', None, 'grp'), may hold values from -6 to 6
- grid_factor: bfloat16 [8192, 896], P(('blk', 'grp')), may hold values from -0.1875 to 0.1875
- metric: float32 [8192, 16, 512], P('blk', 'grp'), may hold values from -0.625 to 0.625
- virt_energy: float32 [896], replicated, may hold values from 0.2 to 4
- pair_energy: float32 [4], replicated, may hold values from -2 to -0.5
Outputs:
- residual: float32 [896, 4, 896], P('blk', None, 'grp')
All inputs are finite; a program needn't handle non-finite values.
Results may differ from a plain program's by a relative error of at most 0.005.
Values may be sent and summed in bfloat16 or wider, within the bound.
A program may use at most 64 MiB of HBM per device.

v0:
```python
import jax
import jax.numpy as jnp
from jax import lax
from jax.sharding import Mesh
from jax.sharding import PartitionSpec as P

GRP = ("grp_0", "grp_1")
BLK_GRP = ("blk", "grp_0", "grp_1")


def from_everyone(x, axis):
    count = lax.axis_size(axis)
    return lax.all_to_all(jnp.broadcast_to(x[None], (count, *x.shape)), axis, 0, 0, tiled=True)


def joined_along(pieces, dim):
    shape = list(pieces.shape[1:])
    shape[dim] *= pieces.shape[0]
    return jnp.moveaxis(pieces, 0, dim).reshape(shape)


def gather_directly(x, axis, dim):
    pieces = from_everyone(x, axis)
    return joined_along(pieces, dim)


def stacked_from(x, axes, sequence):
    pieces = x[None]
    for k in sequence:
        pieces = lax.all_gather(pieces, axes[k], axis=0, tiled=True)
    current = [lax.axis_size(axes[k]) for k in reversed(sequence)]
    pieces = pieces.reshape(*current, *x.shape)
    turned = sorted(range(len(sequence)), key=lambda place: sequence[len(sequence) - 1 - place])
    return pieces.transpose(*turned, *range(len(sequence), pieces.ndim)).reshape(-1, *x.shape)


def gather_axes(x, axes, sequence, dim):
    return joined_along(stacked_from(x, axes, sequence), dim)


def own_block(pieces, axes, sequence):
    shape = [lax.axis_size(a) for a in axes]
    pieces = pieces.reshape(*shape, *pieces.shape[1:])
    pieces = pieces.transpose(*sequence, *range(len(axes), pieces.ndim))
    pieces = pieces.reshape(-1, *pieces.shape[len(axes) :])
    for k in sequence:
        pieces = lax.psum_scatter(pieces, axes[k], scatter_dimension=0, tiled=True)
    return pieces[0]


def cut_along(x, dim, count):
    shape = x.shape
    pieces = x.reshape(*shape[:dim], count, shape[dim] // count, *shape[dim + 1 :])
    return jnp.moveaxis(pieces, dim, 0)


def sum_by_axis(x, axes, sequence, dim):
    count = lax.axis_size(axes)
    return own_block(cut_along(x, dim, count), axes, sequence)


def sent_and_summed(x, axis, dim):
    pieces = cut_along(x, dim, lax.axis_size(axis))
    arrived = lax.all_to_all(pieces, axis, split_axis=0, concat_axis=0, tiled=True)
    return arrived.astype(jnp.float32).sum(axis=0)


def local(amplitudes, grid_factor, metric, virt_energy, pair_energy):
    row_factor = gather_directly(grid_factor, GRP, 0)
    column_factor = gather_directly(grid_factor, "blk", 0)
    amplitude_rows = gather_directly(amplitudes, "blk", 0)
    row_count = row_factor.shape[0]
    left_part = jnp.einsum(
        "pc,ckd->kpd", row_factor, amplitude_rows, preferred_element_type=jnp.float32
    ).astype(jnp.bfloat16)
    columns = column_factor
    products = jnp.einsum(
        "kpd,qd->kpq",
        gather_axes(left_part, GRP, (0, 1), 2),
        columns,
        preferred_element_type=jnp.float32,
    )
    weighted = (metric.reshape(row_count, -1)[None] * products).astype(jnp.bfloat16)
    columns = column_factor
    mixed = (
        sum_by_axis(
            jnp.einsum("kpq,qb->bkp", weighted, columns, preferred_element_type=jnp.float32).astype(
                jnp.bfloat16
            ),
            GRP,
            (1, 0),
            0,
        )
        .astype(jnp.float32)
        .astype(jnp.bfloat16)
    )
    columns = row_factor
    ladder = sent_and_summed(
        jnp.einsum("pa,bkp->akb", columns, mixed, preferred_element_type=jnp.float32).astype(
            jnp.bfloat16
        ),
        "blk",
        0,
    )
    first_energy = lax.dynamic_slice_in_dim(
        virt_energy, lax.axis_index("blk") * amplitudes.shape[0], amplitudes.shape[0]
    )
    second_energy = lax.dynamic_slice_in_dim(
        virt_energy, lax.axis_index(GRP) * amplitudes.shape[2], amplitudes.shape[2]
    )
    denominator = (
        first_energy[:, None, None] + second_energy[None, None, :] - pair_energy[None, :, None]
    )
    return denominator * amplitudes.astype(jnp.float32) + ladder


def solution(mesh):
    split = Mesh(mesh.devices.reshape(mesh.shape["blk"], 2, 8), ("blk", "grp_0", "grp_1"))
    in_specs = (P("blk", None, GRP), P(BLK_GRP, None), P("blk", GRP, None), P(), P())
    out_specs = P("blk", None, GRP)
    return jax.shard_map(local, mesh=split, in_specs=in_specs, out_specs=out_specs, check_vma=False)
```

profile of v0, /device:TPU:1, one launch (start us, length us, event | category | flops | bytes accessed | tf_op | source)
XLA Modules:
  0.0 239.4 jit_solution(6617497980471759122)
XLA Ops:
  6.5 0.9 copy.17
  7.5 0.1 broadcast_bitcast_fusion
  7.6 1.5 reshape.67
  9.1 18.4 %all_to_all.20 = bf16[16,2,6272]{2,1,0:T(2,128)(2,1)S(1)} all-to-all(bf16[16,2,6272]{2,1,0:T(2,128)(2,1)S(1)} %reshape.67), channel_id=1, replica_groups=mesh['blk'=16,'grp_0'=2,'grp_1'=8] {'blk'}, dimensions={0} | all-to-all | bytes 802816 | tf_op jit(solution)/shard_map/all_to_all | solution.py:13
  27.5 1.8 broadcast_in_dim.7
  29.3 8.4 %all-to-all-start.1 = ((bf16[16,32,896]{2,1,0:T(8,128)(2,1)}), bf16[16,32,896]{2,1,0:T(8,128)(2,1)S(1)}, u32[]{:S(2)}, u32[]{:S(2)}) async-start(bf16[16,32,896]{2,1,0:T(8,128)(2,1)} %broadcast_in_dim.7), calls=%async_computation.1 | async-start | bytes 1835008 | tf_op jit(solution)/shard_map/all_to_all | solution.py:13
  37.7 0.0 all-gather.3.cloned.1.call-start
  37.8 1.6 reshape.68
  39.4 0.4 copy.19
  39.8 1.1 reshape.56
  40.9 19.1 %all-to-all-done.1 = bf16[16,32,896]{2,1,0:T(8,128)(2,1)S(1)} async-done(((bf16[16,32,896]{2,1,0:T(8,128)(2,1)}), bf16[16,32,896]{2,1,0:T(8,128)(2,1)S(1)}, u32[]{:S(2)}, u32[]{:S(2)}) %all-to-all-start.1) | async-done | bytes 917536 | tf_op jit(solution)/shard_map/all_to_all | solution.py:13
  60.0 0.5 fusion.1
  60.4 5.6 %all-gather = bf16[8,512,56]{1,2,0:T(8,128)(2,1)} all-gather(bf16[4,512,56]{1,2,0:T(8,128)(2,1)S(1)} %fusion.1), channel_id=2, replica_groups=mesh['blk'=16,'grp_0'=2,'grp_1'=8] {'grp_0'}, dimensions={0}, use_global_device_ids=true | all-gather | bytes 688128 | tf_op jit(solution)/shard_map/all_gather | solution.py:30
  66.1 0.0 all-gather.3.cloned.1.call-update
  66.1 7.9 %all-to-all-start.2 = ((bf16[16,32,896]{2,1,0:T(8,128)(2,1)}), bf16[16,32,896]{2,1,0:T(8,128)(2,1)S(1)}, u32[]{:S(2)}, u32[]{:S(2)}) async-start(bf16[16,32,896]{2,1,0:T(8,128)(2,1)} %broadcast_in_dim.7), calls=%async_computation.2 | async-start | bytes 1835008 | tf_op jit(solution)/shard_map/all_to_all | solution.py:13
  74.0 0.0 reduce-scatter.3.cloned.1.call-start
  74.0 1.3 copy.33
  75.3 40.1 %all-gather.3.cloned.1.call-done = bf16[16,4,512,56]{2,3,1,0:T(8,128)(2,1)} async-done(((bf16[2,4,512,56]{2,3,1,0:T(8,128)(2,1)}), bf16[16,4,512,56]{2,3,1,0:T(8,128)(2,1)}) %all-gather.3.cloned.1.call-update) | async-done | bytes 3670032 | tf_op jit(solution)/shard_map/all_gather | solution.py:30
  115.5 2.3 copy.20
  117.8 2.1 copy.21
  119.8 0.0 all-to-all-done.2
  119.8 7.5 %convert_bitcast_fusion = bf16[896,4,512]{0,2,1:T(8,128)(2,1)} fusion(bf16[512,896,1]{1,0,2:T(8,128)(2,1)S(1)} %bitcast.61, bf16[4,512,896]{1,2,0:T(8,128)(2,1)} %bitcast.56, f32[512,512]{1,0:T(8,128)S(1)} %bitcast.60), kind=kOutput, calls=%fused_computation.1 | convolution fusion | flops 3762028544 | bytes 9306112 | tf_op jit(solution)/shard_map/kpq,qb->bkp/dot_general | solution.py:87
  127.4 5.9 %copy.23 = bf16[896,4,512]{2,0,1:T(8,128)(2,1)} copy(bf16[896,4,512]{0,2,1:T(8,128)(2,1)} %convert_bitcast_fusion) | data formatting | bytes 7340032 | tf_op jit(solution)/shard_map/convert_element_type | solution.py:87
  133.3 4.3 %copy.24 = bf16[8,2,56,4,512]{4,2,3,1,0:T(8,128)(2,1)} copy(bf16[8,2,56,4,512]{4,2,0,1,3:T(8,128)(2,1)} %bitcast.52) | data formatting | bytes 7340032 | tf_op jit(solution)/shard_map/transpose | solution.py:44
  137.6 0.0 reduce-scatter.3.cloned.1.call-update
  137.7 0.0 reduce-scatter.5.cloned.1.call-start
  137.7 49.2 %reduce-scatter.3.cloned.1.call-done = bf16[2,56,4,512]{3,1,2,0:T(8,128)(2,1)} async-done(((bf16[16,56,4,512]{3,1,2,0:T(8,128)(2,1)}), bf16[2,56,4,512]{3,1,2,0:T(8,128)(2,1)}) %reduce-scatter.3.cloned.1.call-update) | async-done | bytes 458768 | tf_op jit(solution)/shard_map/reduce_scatter | solution.py:47
  186.9 0.0 reduce-scatter.5.cloned.1.call-update
  186.9 20.5 %reduce-scatter.5.cloned.1.call-done = bf16[1,56,4,512]{3,1,2,0:T(8,128)(2,1)} async-done(((bf16[2,56,4,512]{3,1,2,0:T(8,128)(2,1)}), bf16[1,56,4,512]{3,1,2,0:T(8,128)(2,1)}) %reduce-scatter.5.cloned.1.call-update) | async-done | bytes 229392 | tf_op jit(solution)/shard_map/reduce_scatter | solution.py:47
  207.4 1.4 fusion
  208.8 0.0 copy-start
  208.8 1.5 reshape.63
  210.3 0.2 copy.34
  210.5 2.2 reshape.69
  212.7 7.2 %all-to-all-start.3 = ((bf16[16,2,6272]{2,1,0:T(2,128)(2,1)}), bf16[16,2,6272]{2,1,0:T(2,128)(2,1)S(1)}, u32[]{:S(2)}, u32[]{:S(2)}) async-start(bf16[16,2,6272]{2,1,0:T(2,128)(2,1)} %reshape.69), calls=%async_computation.5 | async-start | bytes 802816 | tf_op jit(solution)/shard_map/all_to_all | solution.py:64
  220.0 0.8 fusion.3
  220.8 0.1 broadcast_add_fusion
  220.9 9.3 %all-to-all-done.3 = bf16[16,2,6272]{2,1,0:T(2,128)(2,1)S(1)} async-done(((bf16[16,2,6272]{2,1,0:T(2,128)(2,1)}), bf16[16,2,6272]{2,1,0:T(2,128)(2,1)S(1)}, u32[]{:S(2)}, u32[]{:S(2)}) %all-to-all-start.3) | async-done | bytes 401440 | tf_op jit(solution)/shard_map/all_to_all | solution.py:64
  230.2 1.6 reshape.70
  231.8 0.2 convert_reduce_fusion
  232.0 0.0 copy-done
  232.0 0.1 multiply_add_fusion
  232.1 0.7 copy.27
Async XLA Ops:
  29.3 30.7 %all-to-all-start.1 = ((bf16[16,32,896]{2,1,0:T(8,128)(2,1)}), bf16[16,32,896]{2,1,0:T(8,128)(2,1)S(1)}, u32[]{:S(2)}, u32[]{:S(2)}) async-start(bf16[16,32,896]{2,1,0:T(8,128)(2,1)} %broadcast_in_dim.7), calls=%async_computation.1 | async-start | bytes 1835008 | tf_op jit(solution)/shard_map/all_to_all | solution.py:13
  37.7 77.8 %all-gather.3.cloned.1.call-start = ((), (), s32[]{:S(2)}) async-start(), calls=%async_computation.6 | async-start | bytes 4128768 | tf_op jit(solution)/shard_map/all_gather | solution.py:30
  66.1 53.7 %all-to-all-start.2 = ((bf16[16,32,896]{2,1,0:T(8,128)(2,1)}), bf16[16,32,896]{2,1,0:T(8,128)(2,1)S(1)}, u32[]{:S(2)}, u32[]{:S(2)}) async-start(bf16[16,32,896]{2,1,0:T(8,128)(2,1)} %broadcast_in_dim.7), calls=%async_computation.2 | async-start | bytes 1835008 | tf_op jit(solution)/shard_map/all_to_all | solution.py:13
  74.0 112.9 %reduce-scatter.3.cloned.1.call-start = ((), (), s32[]{:S(2)}) async-start(), calls=%async_computation.7 | async-start | bytes 4128768 | tf_op jit(solution)/shard_map/reduce_scatter | solution.py:47
  137.7 69.8 %reduce-scatter.5.cloned.1.call-start = ((), (), s32[]{:S(2)}) async-start(), calls=%async_computation.8 | async-start | bytes 688128 | tf_op jit(solution)/shard_map/reduce_scatter | solution.py:47
  208.8 23.2 %copy-start = (f32[4]{0:T(128)S(1)}, f32[4]{0:T(128)}, u32[]{:S(2)}) copy-start(f32[4]{0:T(128)} %param.9) | copy-start | bytes 52
  212.7 17.4 %all-to-all-start.3 = ((bf16[16,2,6272]{2,1,0:T(2,128)(2,1)}), bf16[16,2,6272]{2,1,0:T(2,128)(2,1)S(1)}, u32[]{:S(2)}, u32[]{:S(2)}) async-start(bf16[16,2,6272]{2,1,0:T(2,128)(2,1)} %reshape.69), calls=%async_computation.5 | async-start | bytes 802816 | tf_op jit(solution)/shard_map/all_to_all | solution.py:64
Sparse Core Ops, SparseCore 0:
  66.2 49.2 all-gather.2
  137.8 49.0 reduce-scatter.2
  189.4 17.9 reduce-scatter.4
where the time goes:
time: 240 us; the launch traced here: 239 us
  waiting for transfers between devices  138 us (58%)
  local copies, waits for them, and re-layouts  30.5 us (13%)
  blocking collectives  24 us (10%)
  starting transfers between devices  23.7 us (10%)
  between operations  13.2 us (6%)
  matrix products  9.37 us (4%)
    reduce_scatter x2, waiting for transfers between devices, own_block(): pieces = lax.psum_scatter(pieces, axes[k], scatter_dimension=0, tiled=True)  69.7 us
    all_gather x1, waiting for transfers between devices, stacked_from(): pieces = lax.all_gather(pieces, axes[k], axis=0, tiled=True)  40.1 us
    all_to_all x2, waiting for transfers between devices, from_everyone(): lax.all_to_all(jnp.broadcast_to(x[None], (count, *x.shape)), axis, 0, 0,...  19.1 us
    all_to_all x1, blocking collectives, from_everyone(): lax.all_to_all(jnp.broadcast_to(x[None], (count, *x.shape)), axis, 0, 0,...  18.4 us
    all_to_all x2, starting transfers between devices, from_everyone(): lax.all_to_all(jnp.broadcast_to(x[None], (count, *x.shape)), axis, 0, 0,...  16.3 us
    unnamed x9, local copies, waits for them, and re-layouts  9.32 us
    all_to_all x1, waiting for transfers between devices, sent_and_summed(): lax.all_to_all(pieces, axis, split_axis=0, concat_axis=0, tiled=True)  9.27 us
    dot_general x1, matrix products, local(): jnp.einsum('kpq,qb->bkp', weighted, columns, preferred_element_type=jnp.f...  7.54 us
  transfers between devices with their start and end apart: 6, of which 5 were waited for; matrix products, arithmetic and copies ran while one was open for 4% of the time, Pallas kernels for 0%

commit v1 on v0

--- a/solution.py
+++ b/solution.py
@@ -27,7 +27,9 @@
 def stacked_from(x, axes, sequence):
     pieces = x[None]
     for k in sequence:
-        pieces = lax.all_gather(pieces, axes[k], axis=0, tiled=True)
+        pieces = jnp.concatenate(
+            lax.all_to_all(jnp.stack([pieces] * lax.axis_size(axes[k])), axes[k], 0, 0), axis=0
+        )
     current = [lax.axis_size(axes[k]) for k in reversed(sequence)]
     pieces = pieces.reshape(*current, *x.shape)
     turned = sorted(range(len(sequence)), key=lambda place: sequence[len(sequence) - 1 - place])

time: 240 us -> 297 us (1.24)
  blocking collectives: 24 us -> 115 us
  waiting for transfers between devices: 138 us -> 103 us
    all_to_all x0 -> x2, blocking collectives: none -> 96.5 us  [stacked_from(): lax.all_to_all(jnp.stack([pieces] * lax.axis_size(axes[k])), axes[k], 0, 0)]
    all_gather x1 -> x0, waiting for transfers between devices: 40.1 us -> none  [stacked_from(): pieces = lax.all_gather(pieces, axes[k], axis=0, tiled=True)]
    all_to_all x2, waiting for transfers between devices: 19.1 us -> 30.2 us  [from_everyone(): lax.all_to_all(jnp.broadcast_to(x[None], (count, *x.shape)), axis, 0, 0,...]
    reduce_scatter x2, waiting for transfers between devices: 69.7 us -> 63.4 us  [own_block(): pieces = lax.psum_scatter(pieces, axes[k], scatter_dimension=0, tiled=True)]
    all_gather x1 -> x0, blocking collectives: 5.64 us -> none  [stacked_from(): pieces = lax.all_gather(pieces, axes[k], axis=0, tiled=True)]
    unnamed x9 -> x11, local copies, waits for them, and re-layouts: 9.32 us -> 8.12 us
  transfers between devices with their start and end apart: 6 -> 5, of which waited for: 5 -> 5; matrix products, arithmetic and copies ran while one was open for 4% -> 3% of each run, Pallas kernels for 0% -> 0%
where the time goes in v1:
time: 297 us; the launch traced here: 296 us
  blocking collectives  115 us (39%)
  waiting for transfers between devices  103 us (35%)
  local copies, waits for them, and re-layouts  29.6 us (10%)
  starting transfers between devices  23.7 us (8%)
  between operations  13.6 us (5%)
  matrix products  10.8 us (4%)
    all_to_all x2, blocking collectives, stacked_from(): lax.all_to_all(jnp.stack([pieces] * lax.axis_size(axes[k])), axes[k], 0, 0)  96.5 us
    reduce_scatter x2, waiting for transfers between devices, own_block(): pieces = lax.psum_scatter(pieces, axes[k], scatter_dimension=0, tiled=True)  63.4 us
    all_to_all x2, waiting for transfers between devices, from_everyone(): lax.all_to_all(jnp.broadcast_to(x[None], (count, *x.shape)), axis, 0, 0,...  30.2 us
    all_to_all x1, blocking collectives, from_everyone(): lax.all_to_all(jnp.broadcast_to(x[None], (count, *x.shape)), axis, 0, 0,...  18.4 us
    all_to_all x2, starting transfers between devices, from_everyone(): lax.all_to_all(jnp.broadcast_to(x[None], (count, *x.shape)), axis, 0, 0,...  16.2 us
    all_to_all x1, waiting for transfers between devices, sent_and_summed(): lax.all_to_all(pieces, axis, split_axis=0, concat_axis=0, tiled=True)  9.27 us
    dot_general x1, matrix products, local(): jnp.einsum('kpq,qb->bkp', weighted, columns, preferred_element_type=jnp.f...  8.97 us
    unnamed x11, local copies, waits for them, and re-layouts  8.12 us
  transfers between devices with their start and end apart: 5, of which 5 were waited for; matrix products, arithmetic and copies ran while one was open for 3% of the time, Pallas kernels for 0%

profile of v1, /device:TPU:1, one launch (start us, length us, event | category | flops | bytes accessed | tf_op | source)
XLA Modules:
  0.0 296.0 jit_solution(8276190530892608864)
XLA Ops:
  6.5 0.9 copy.17
  7.5 0.1 broadcast_bitcast_fusion
  7.6 1.5 reshape.64
  9.1 18.4 %all_to_all.30 = bf16[16,2,6272]{2,1,0:T(2,128)(2,1)S(1)} all-to-all(bf16[16,2,6272]{2,1,0:T(2,128)(2,1)S(1)} %reshape.64), channel_id=1, replica_groups=mesh['blk'=16,'grp_0'=2,'grp_1'=8] {'blk'}, dimensions={0} | all-to-all | bytes 802816 | tf_op jit(solution)/shard_map/all_to_all | solution.py:13
  27.5 1.8 broadcast_in_dim.5
  29.3 8.4 %all-to-all-start.1 = ((bf16[16,32,896]{2,1,0:T(8,128)(2,1)}), bf16[16,32,896]{2,1,0:T(8,128)(2,1)S(1)}, u32[]{:S(2)}, u32[]{:S(2)}) async-start(bf16[16,32,896]{2,1,0:T(8,128)(2,1)} %broadcast_in_dim.5), calls=%async_computation.1 | async-start | bytes 1835008 | tf_op jit(solution)/shard_map/all_to_all | solution.py:13
  37.7 1.6 reshape.65
  39.3 0.4 copy.19
  39.7 1.1 reshape.55
  40.8 19.1 %all-to-all-done.1 = bf16[16,32,896]{2,1,0:T(8,128)(2,1)S(1)} async-done(((bf16[16,32,896]{2,1,0:T(8,128)(2,1)}), bf16[16,32,896]{2,1,0:T(8,128)(2,1)S(1)}, u32[]{:S(2)}, u32[]{:S(2)}) %all-to-all-start.1) | async-done | bytes 917536 | tf_op jit(solution)/shard_map/all_to_all | solution.py:13
  59.9 0.5 fusion.1
  60.5 7.5 %all_to_all.31 = bf16[2,1,4,512,56]{3,4,2,1,0:T(8,128)(2,1)S(1)} all-to-all(bf16[2,1,4,512,56]{3,4,2,1,0:T(8,128)(2,1)S(1)} %pad_maximum_fusion), channel_id=1, replica_groups=mesh['blk'=16,'grp_0'=2,'grp_1'=8] {'grp_0'}, dimensions={0} | all-to-all | bytes 917504 | tf_op jit(solution)/shard_map/all_to_all | solution.py:31
  68.0 0.4 stack.7
  68.3 0.0 copy-start
  68.3 89.1 %all_to_all.32 = bf16[8,2,4,512,56]{3,4,2,1,0:T(8,128)(2,1)} all-to-all(bf16[8,2,4,512,56]{3,4,2,1,0:T(8,128)(2,1)S(1)} %stack.7), channel_id=1, replica_groups=mesh['blk'=16,'grp_0'=2,'grp_1'=8] {'grp_1'}, dimensions={0} | all-to-all | bytes 7340032 | tf_op jit(solution)/shard_map/all_to_all | solution.py:31
  157.4 7.8 %all-to-all-start.4 = ((bf16[16,32,896]{2,1,0:T(8,128)(2,1)}), bf16[16,32,896]{2,1,0:T(8,128)(2,1)}, u32[]{:S(2)}, u32[]{:S(2)}) async-start(bf16[16,32,896]{2,1,0:T(8,128)(2,1)} %broadcast_in_dim.5), calls=%async_computation.4 | async-start | bytes 1835008 | tf_op jit(solution)/shard_map/all_to_all | solution.py:13
  165.2 0.0 reduce-scatter.3.cloned.1.call-start
  165.3 0.0 copy-done
  165.3 0.1 copy.33
  165.3 2.3 copy.20
  167.6 2.1 copy.21
  169.7 11.1 %all-to-all-done.4 = bf16[16,32,896]{2,1,0:T(8,128)(2,1)} async-done(((bf16[16,32,896]{2,1,0:T(8,128)(2,1)}), bf16[16,32,896]{2,1,0:T(8,128)(2,1)}, u32[]{:S(2)}, u32[]{:S(2)}) %all-to-all-start.4) | async-done | bytes 917536 | tf_op jit(solution)/shard_map/all_to_all | solution.py:13
  180.8 9.0 %convert_bitcast_fusion = bf16[896,4,512]{0,2,1:T(8,128)(2,1)} fusion(bf16[512,896,1]{1,0,2:T(8,128)(2,1)} %bitcast.10, bf16[4,512,896]{1,2,0:T(8,128)(2,1)} %bitcast.56, f32[512,512]{1,0:T(8,128)S(1)} %bitcast.60), kind=kOutput, calls=%fused_computation.1 | convolution fusion | flops 3762028544 | bytes 9306112 | tf_op jit(solution)/shard_map/kpq,qb->bkp/dot_general | solution.py:89
  189.8 5.9 %copy.23 = bf16[896,4,512]{2,0,1:T(8,128)(2,1)} copy(bf16[896,4,512]{0,2,1:T(8,128)(2,1)} %convert_bitcast_fusion) | data formatting | bytes 7340032 | tf_op jit(solution)/shard_map/convert_element_type | solution.py:89
  195.7 4.3 %copy.24 = bf16[8,2,56,4,512]{4,2,3,1,0:T(8,128)(2,1)} copy(bf16[8,2,56,4,512]{4,2,0,1,3:T(8,128)(2,1)} %bitcast.53) | data formatting | bytes 7340032 | tf_op jit(solution)/shard_map/transpose | solution.py:46
  200.0 0.0 reduce-scatter.3.cloned.1.call-update
  200.1 0.2 reduce-scatter.5.cloned.1.call-start
  200.3 43.0 %reduce-scatter.3.cloned.1.call-done = bf16[2,56,4,512]{3,1,2,0:T(8,128)(2,1)} async-done(((bf16[16,56,4,512]{3,1,2,0:T(8,128)(2,1)}), bf16[2,56,4,512]{3,1,2,0:T(8,128)(2,1)}) %reduce-scatter.3.cloned.1.call-update) | async-done | bytes 458768 | tf_op jit(solution)/shard_map/reduce_scatter | solution.py:49
  243.2 0.0 reduce-scatter.5.cloned.1.call-update
  243.3 20.5 %reduce-scatter.5.cloned.1.call-done = bf16[1,56,4,512]{3,1,2,0:T(8,128)(2,1)} async-done(((bf16[2,56,4,512]{3,1,2,0:T(8,128)(2,1)}), bf16[1,56,4,512]{3,1,2,0:T(8,128)(2,1)}) %reduce-scatter.5.cloned.1.call-update) | async-done | bytes 229392 | tf_op jit(solution)/shard_map/reduce_scatter | solution.py:49
  263.7 1.4 fusion
  265.1 0.0 copy-start.1
  265.1 1.5 reshape.61
  266.6 0.2 copy.34
  266.8 2.2 reshape.66
  269.1 7.2 %all-to-all-start.5 = ((bf16[16,2,6272]{2,1,0:T(2,128)(2,1)}), bf16[16,2,6272]{2,1,0:T(2,128)(2,1)S(1)}, u32[]{:S(2)}, u32[]{:S(2)}) async-start(bf16[16,2,6272]{2,1,0:T(2,128)(2,1)} %reshape.66), calls=%async_computation.7 | async-start | bytes 802816 | tf_op jit(solution)/shard_map/all_to_all | solution.py:66
  276.3 0.8 fusion.3
  277.2 0.1 broadcast_add_fusion
  277.2 9.3 %all-to-all-done.5 = bf16[16,2,6272]{2,1,0:T(2,128)(2,1)S(1)} async-done(((bf16[16,2,6272]{2,1,0:T(2,128)(2,1)}), bf16[16,2,6272]{2,1,0:T(2,128)(2,1)S(1)}, u32[]{:S(2)}, u32[]{:S(2)}) %all-to-all-start.5) | async-done | bytes 401440 | tf_op jit(solution)/shard_map/all_to_all | solution.py:66
  286.5 1.6 reshape.67
  288.1 0.2 convert_reduce_fusion
  288.3 0.0 copy-done.1
  288.3 0.1 multiply_add_fusion
  288.4 0.7 copy.27
  (1 shorter events, 0.0 us)
Async XLA Ops:
  29.3 30.7 %all-to-all-start.1 = ((bf16[16,32,896]{2,1,0:T(8,128)(2,1)}), bf16[16,32,896]{2,1,0:T(8,128)(2,1)S(1)}, u32[]{:S(2)}, u32[]{:S(2)}) async-start(bf16[16,32,896]{2,1,0:T(8,128)(2,1)} %broadcast_in_dim.5), calls=%async_computation.1 | async-start | bytes 1835008 | tf_op jit(solution)/shard_map/all_to_all | solution.py:13
  68.3 96.9 %copy-start = (f32[512,1,512]{2,1,0:T(1,128)S(1)}, f32[512,1,512]{2,1,0:T(1,128)}, u32[]{:S(2)}) copy-start(f32[512,1,512]{2,1,0:T(1,128)} %param.7) | copy-start | bytes 3145732
  157.4 23.4 %all-to-all-start.4 = ((bf16[16,32,896]{2,1,0:T(8,128)(2,1)}), bf16[16,32,896]{2,1,0:T(8,128)(2,1)}, u32[]{:S(2)}, u32[]{:S(2)}) async-start(bf16[16,32,896]{2,1,0:T(8,128)(2,1)} %broadcast_in_dim.5), calls=%async_computation.4 | async-start | bytes 1835008 | tf_op jit(solution)/shard_map/all_to_all | solution.py:13
  165.2 78.0 %reduce-scatter.3.cloned.1.call-start = ((), (), s32[]{:S(2)}) async-start(), calls=%async_computation.8 | async-start | bytes 4128768 | tf_op jit(solution)/shard_map/reduce_scatter | solution.py:49
  200.1 63.7 %reduce-scatter.5.cloned.1.call-start = ((), (), s32[]{:S(2)}) async-start(), calls=%async_computation.9 | async-start | bytes 688128 | tf_op jit(solution)/shard_map/reduce_scatter | solution.py:49
  265.1 23.2 %copy-start.1 = (f32[4]{0:T(128)S(1)}, f32[4]{0:T(128)}, u32[]{:S(2)}) copy-start(f32[4]{0:T(128)} %param.9) | copy-start | bytes 52
  269.1 17.4 %all-to-all-start.5 = ((bf16[16,2,6272]{2,1,0:T(2,128)(2,1)}), bf16[16,2,6272]{2,1,0:T(2,128)(2,1)S(1)}, u32[]{:S(2)}, u32[]{:S(2)}) async-start(bf16[16,2,6272]{2,1,0:T(2,128)(2,1)} %reshape.66), calls=%async_computation.7 | async-start | bytes 802816 | tf_op jit(solution)/shard_map/all_to_all | solution.py:66
Sparse Core Ops, SparseCore 0:
  200.2 43.0 reduce-scatter.2
  245.8 17.9 reduce-scatter.4
